TPU v7x, 256 devices: a whole 4x4x8 slice. The times are simulated.
256 devices in a mesh: seq: 64 (over y, z_lo, x), tp: 4 (over z_hi, core).
Axes of the slice: x: 4, y: 4, z: 8 (z_hi: 2, z_lo: 4; z = z_hi * 4 + z_lo), core: 2. Of those that a mesh axis runs over, the one named last changes fastest.
Arguments:
- hidden_in: bfloat16 [16384, 4096], P('seq', 'tp'), may hold values from -6 to 6
- order: int32 [16384], P('seq'), may hold values from 0 to 16383, as said below
- segment: int32 [16384], replicated, may hold values from 0 to 31, never falling along the last dimension, each value on 1 to 2048 neighbouring positions
- norm_gain: float32 [4096], replicated, may hold values from 0.1 to 1.9
- w_query: bfloat16 [4096, 2048], P('seq', 'tp')
- w_key: bfloat16 [4096, 512], P('seq', 'tp'), may hold values from -0.09375 to 0.09375
- w_value: bfloat16 [4096, 512], P('seq', 'tp'), may hold values from -0.09375 to 0.09375
- w_out: bfloat16 [2048, 4096], P('seq', 'tp'), may hold values from -0.5 to 0.5
Outputs:
- attn_out: bfloat16 [16384, 4096], P('seq', 'tp')
Inputs may be any that keep to these rules, and one draw needn't show every extreme that they name: order holds every position once; it is made of runs of 64 consecutive positions, each starting at a multiple of 64 and stored in rows that start at a multiple of 64. `segment`: never falls along positions.
All inputs are finite; a program needn't handle non-finite values.
Results may differ from a plain program's by a relative error of at most 0.014.
The roundings to bfloat16 on the way count: a program that leaves them out, or rounds other values in their place, can miss the bound.
Values may be sent and summed in bfloat16 or wider, within the bound.
No kernel may reach another device: no remote copies, remote signals or barrier semaphores. Data moves between devices by JAX's collectives and lax.ppermute only.
A program may use at most 128 MiB of HBM per device.

v0:
```python
import jax
import jax.numpy as jnp
from jax import lax
from jax.sharding import Mesh
from jax.sharding import PartitionSpec as P

HD = 128
SEQ = ("seq_0", "seq_1", "seq_2")
THETA = 500000.0
EPS = 1e-05


def sent_to_all(array, axis):
    copies = jnp.broadcast_to(array, (lax.axis_size(axis), *array.shape))
    return lax.all_to_all(copies, axis, split_axis=0, concat_axis=0, tiled=True)


def joined_along(blocks, dim):
    blocks = jnp.moveaxis(blocks, 0, dim)
    dims = blocks.shape
    return blocks.reshape(*dims[:dim], dims[dim] * dims[dim + 1], *dims[dim + 2 :])


def gather_directly(array, axis, dim):
    blocks = sent_to_all(array, axis)
    return joined_along(blocks, dim)


def side_by_side(arrays, axis, dim, along):
    widths = [a.shape[along] for a in arrays]
    both = jnp.concatenate(arrays, axis=along)
    filled = lax.all_gather(both, axis, axis=dim, tiled=True)
    return tuple(jnp.split(filled, [sum(widths[:k]) for k in range(1, len(widths))], axis=along))


def stacked_from(array, axes, sequence):
    blocks = array
    for k in sequence:
        blocks = lax.all_gather(blocks, axes[k])
    done = sequence[::-1]
    back = [done.index(k) for k in range(len(axes))]
    blocks = blocks.transpose(*back, *range(len(axes), blocks.ndim))
    return blocks.reshape(-1, *array.shape)


def gathered_by_axis(array, axes, sequence, dim):
    return joined_along(stacked_from(array, axes, sequence), dim)


def rotary(block, positions):
    head_dim = block.shape[-1]
    width = head_dim // 2
    frequency = THETA ** (-jnp.arange(width, dtype=jnp.float32) * 2.0 / head_dim)
    angle = positions.astype(jnp.float32)[:, None] * frequency[None, :]
    cosine = jnp.cos(angle)[:, None, :]
    sine = jnp.sin(angle)[:, None, :]
    first = block[..., :width]
    second = block[..., width:]
    return jnp.concatenate(
        [first * cosine - second * sine, second * cosine + first * sine], axis=-1
    )


def on_device(hidden_in, order, segment, norm_gain, w_query, w_key, w_value, w_out):
    rows = hidden_in.shape[0]
    whole = gather_directly(hidden_in, "tp", 1)
    wide = whole.astype(jnp.float32)
    mean_square = jnp.mean(wide * wide, axis=1, keepdims=True)
    normed = (wide * lax.rsqrt(mean_square + EPS) * norm_gain[None, :]).astype(jnp.bfloat16)
    pieces = side_by_side((w_query, w_key, w_value), SEQ, 0, 1)
    columns = normed
    query, key, value = tuple(
        (jnp.dot(columns, piece, preferred_element_type=jnp.float32) for piece in pieces)
    )
    heads_local = w_query.shape[1] // HD
    groups_local = w_key.shape[1] // HD
    group = heads_local // groups_local
    query = (rotary(query.reshape(rows, heads_local, HD), order) * HD ** (-0.5)).astype(
        jnp.bfloat16
    )
    query = query.reshape(rows, groups_local, group, HD)
    key = rotary(key.reshape(rows, groups_local, HD), order).astype(jnp.bfloat16)
    value = value.reshape(rows, groups_local, HD).astype(jnp.bfloat16)
    document = jnp.take(segment, order, axis=0)

    def attend(carry, block):
        key_block, value_block, key_order, key_document = block
        allowed = (key_order[None, :] <= order[:, None]) & (
            key_document[None, :] == document[:, None]
        )
        maximum, total, weighted = carry
        scores = jnp.einsum("rkgd,ckd->rkgc", query, key_block, preferred_element_type=jnp.float32)
        scores = jnp.where(allowed[:, None, None, :], scores, -jnp.inf)
        new_max = jnp.maximum(maximum, jnp.max(scores, axis=-1))
        anchor = jnp.where(new_max == -jnp.inf, 0.0, new_max)
        weights = jnp.exp(scores - anchor[..., None])
        shrink = jnp.exp(maximum - anchor)
        total = total * shrink + jnp.sum(weights, axis=-1)
        weighted = weighted * shrink[..., None] + jnp.einsum(
            "rkgc,ckd->rkgd",
            weights.astype(jnp.bfloat16),
            value_block,
            preferred_element_type=jnp.float32,
        )
        return (new_max, total, weighted)

    initial = (
        jnp.full((rows, groups_local, group), -jnp.inf, jnp.float32),
        jnp.zeros((rows, groups_local, group), jnp.float32),
        jnp.zeros((rows, groups_local, group, HD), jnp.float32),
    )
    carry = initial
    piece = (
        *side_by_side((key, value), SEQ, 0, 1),
        lax.all_gather(order, SEQ, axis=0, tiled=True),
        lax.all_gather(document, SEQ, axis=0, tiled=True),
    )
    count = piece[0].shape[0]
    stacked = tuple((member.reshape((count // 512, 512) + member.shape[1:]) for member in piece))
    carry, unused = lax.scan(lambda state, block: (attend(state, block), None), carry, stacked)
    maximum, total, weighted = carry
    mixed = (weighted / total[..., None]).reshape(rows, heads_local * HD).astype(jnp.bfloat16)
    every_head = gather_directly(mixed, "tp", 1)
    piece = gathered_by_axis(w_out, SEQ, (1, 0, 2), 0)
    columns = every_head
    result = jnp.dot(columns, piece, preferred_element_type=jnp.float32)
    return result.astype(jnp.bfloat16)


def solution(mesh):
    torus = Mesh(mesh.devices.reshape(4, 4, 4, mesh.shape["tp"]), ("seq_0", "seq_1", "seq_2", "tp"))
    placed = (
        P(SEQ, "tp"),
        P(SEQ),
        P(),
        P(),
        P(SEQ, "tp"),
        P(SEQ, "tp"),
        P(SEQ, "tp"),
        P(SEQ, "tp"),
    )
    return jax.shard_map(
        on_device, mesh=torus, in_specs=placed, out_specs=P(SEQ, "tp"), check_vma=False
    )
```

profile of v0, /device:TPU:1, one launch (start us, length us, event | category | flops | bytes accessed | tf_op | source)
XLA Modules:
  0.0 937.8 jit_solution(4467411417672132659)
XLA Ops:
  6.5 1.6 pad_maximum_fusion.1
  8.1 2.6 broadcast_in_dim.58
  10.8 9.9 %all-to-all-start = ((bf16[4,256,1024]{2,1,0:T(8,128)(2,1)}), bf16[4,256,1024]{2,1,0:T(8,128)(2,1)}, u32[]{:S(2)}, u32[]{:S(2)}) async-start(bf16[4,256,1024]{2,1,0:T(8,128)(2,1)} %broadcast_in_dim.58), calls=%async_computation | async-start | bytes 4194304 | tf_op jit(solution)/shard_map/all_to_all | solution.py:15
  20.7 67.4 %all-gather = bf16[128,1024]{1,0:T(8,128)(2,1)} all-gather(bf16[32,1024]{1,0:T(8,128)(2,1)S(1)} %copy-done.5), channel_id=2, replica_groups=mesh['seq_0'=4,'seq_1'=4,'seq_2'=4,'tp'=4] {'seq_1'}, dimensions={0}, use_global_device_ids=true | all-gather | bytes 327680 | tf_op jit(solution)/shard_map/all_gather | solution.py:39
  88.3 1.7 gather_fusion
  90.0 2.9 copy.37
  93.5 1.7 fusion.21
  95.2 248.8 %all-gather.10.cloned.1.call-done = bf16[4096,768]{1,0:T(8,128)(2,1)} async-done(((bf16[64,768]{1,0:T(8,128)(2,1)}), bf16[4096,768]{1,0:T(8,128)(2,1)}) %all-gather.10.cloned.1.call-update) | async-done | bytes 6291472 | tf_op jit(solution)/shard_map/all_gather | solution.py:32
  344.0 2.4 convolution_bitcast_fusion.1
  346.7 2.4 fusion.22
  349.9 159.7 %all-gather.4 = s32[64,1,256]{2,1,0:T(1,128)S(1)} all-gather(s32[1,1,256]{2,1,0:T(1,128)S(1)} %bitcast.141), channel_id=1, replica_groups=mesh['seq_0'=4,'seq_1'=4,'seq_2'=4,'tp'=4] {'seq_0','seq_1','seq_2'}, dimensions={0}, use_global_device_ids=true | all-gather | bytes 66560 | tf_op jit(solution)/shard_map/all_gather | solution.py:116
  509.8 155.2 %all-gather.3 = s32[64,1,256]{2,1,0:T(1,128)S(1)} all-gather(s32[1,1,256]{2,1,0:T(1,128)S(1)} %bitcast.140), channel_id=1, replica_groups=mesh['seq_0'=4,'seq_1'=4,'seq_2'=4,'tp'=4] {'seq_0','seq_1','seq_2'}, dimensions={0}, use_global_device_ids=true | all-gather | bytes 66560 | tf_op jit(solution)/shard_map/all_gather | solution.py:115
  665.6 1.7 multiply_convert_fusion
  667.3 4.5 slice_bitcast_fusion
  671.8 6.6 copy.39
  678.4 3.4 fusion.36
  682.2 5.1 fusion.34
  687.3 2.5 copy.52
  689.8 6.4 copy.48
  696.2 117.0 %while.15 = (s32[]{:T(128)}, f32[256,1,4]{0,2,1:T(4,128)S(1)}, f32[256,1,4]{0,2,1:T(4,128)S(1)}, f32[256,1,4,128]{0,3,2,1:T(8,128)S(1)}, s32[32,512]{1,0:T(8,128...) while((s32[]{:T(128)}, f32[256,1,4]{0,2,1:T(4,128)S(1)}, ...), condition=%wide.region_4.5_spmd.clone, body=%wide.region_1.4_spmd.clone.sunk | while | flops 273428480 | bytes 8476829 | solution.py:120
  698.2 1.6 fusion.56
  701.9 1.6 fusion.56
  705.6 1.6 fusion.56
  709.2 1.6 fusion.56
  711.1 1.4 fusion.52
  712.9 1.6 fusion.56
  716.5 1.6 fusion.56
  720.2 1.6 fusion.56
  723.8 1.6 fusion.56
  725.7 1.4 fusion.52
  727.5 1.6 fusion.56
  731.2 1.6 fusion.56
  734.8 1.6 fusion.56
  738.5 1.6 fusion.56
  740.3 1.4 fusion.52
  742.1 1.6 fusion.56
  745.8 1.6 fusion.56
  749.4 1.6 fusion.56
  753.1 1.6 fusion.56
  756.8 1.6 fusion.56
  760.4 1.6 fusion.56
  762.3 1.4 fusion.52
  764.1 1.6 fusion.56
  766.0 1.4 fusion.52
  767.8 1.6 fusion.56
  771.4 1.6 fusion.56
  773.3 1.4 fusion.52
  775.1 1.6 fusion.56
  777.0 1.4 fusion.52
  778.7 1.6 fusion.56
  782.4 1.6 fusion.56
  786.1 1.6 fusion.56
  787.9 1.4 fusion.52
  789.7 1.6 fusion.56
  793.4 1.6 fusion.56
  797.0 1.6 fusion.56
  800.7 1.6 fusion.56
  804.4 1.6 fusion.56
  808.0 1.6 fusion.56
  811.7 1.6 fusion.56
  814.4 95.3 %all-to-all-start.1 = ((bf16[4,256,512]{1,2,0:T(8,128)(2,1)}), bf16[4,256,512]{1,2,0:T(8,128)(2,1)S(1)}, u32[]{:S(2)}, u32[]{:S(2)}) async-start(bf16[4,256,512]{1,2,0:T(8,128)(2,1)} %broadcast_in_dim.59), calls=%async_computation.1 | async-start | bytes 2097152 | tf_op jit(solution)/shard_map/all_to_all | solution.py:15
  909.7 5.0 copy.44
  914.7 12.4 %all-to-all-done.1 = bf16[4,256,512]{1,2,0:T(8,128)(2,1)S(1)} async-done(((bf16[4,256,512]{1,2,0:T(8,128)(2,1)}), bf16[4,256,512]{1,2,0:T(8,128)(2,1)S(1)}, u32[]{:S(2)}, u32[]{:S(2)}) %all-to-all-start.1) | async-done | bytes 1048608 | tf_op jit(solution)/shard_map/all_to_all | solution.py:15
  927.0 4.3 convolution_convert_fusion
  (294 shorter events, 57.3 us)
Async XLA Ops:
  6.5 81.7 %copy-start = (s32[16384]{0:T(1024)S(1)}, s32[16384]{0:T(1024)}, u32[]{:S(2)}) copy-start(s32[16384]{0:T(1024)} %param.12) | copy-start | bytes 196612
  6.5 14.2 %copy-start.5 = (bf16[32,1024]{1,0:T(8,128)(2,1)S(1)}, bf16[32,1024]{1,0:T(8,128)(2,1)}, u32[]{:S(2)}) copy-start(bf16[32,1024]{1,0:T(8,128)(2,1)} %param.17) | copy-start | bytes 196612
  6.5 81.7 %copy-start.3 = (s32[256]{0:T(256)S(1)}, s32[256]{0:T(256)}, u32[]{:S(2)}) copy-start(s32[256]{0:T(256)} %param.11) | copy-start | bytes 3076
  6.5 337.4 %all-gather.10.cloned.1.call-start = ((), (), s32[]{:S(2)}) async-start(), calls=%async_computation.2 | async-start | bytes 6389760 | tf_op jit(solution)/shard_map/all_gather | solution.py:32
  10.8 79.2 %all-to-all-start = ((bf16[4,256,1024]{2,1,0:T(8,128)(2,1)}), bf16[4,256,1024]{2,1,0:T(8,128)(2,1)}, u32[]{:S(2)}, u32[]{:S(2)}) async-start(bf16[4,256,1024]{2,1,0:T(8,128)(2,1)} %broadcast_in_dim.58), calls=%async_computation | async-start | bytes 4194304 | tf_op jit(solution)/shard_map/all_to_all | solution.py:15
  20.7 72.8 %copy-start.4 = (f32[4096]{0:T(1024)S(1)}, f32[4096]{0:T(1024)}, u32[]{:S(2)}) copy-start(f32[4096]{0:T(1024)} %param.13) | copy-start | bytes 49156
  20.7 644.9 %all-gather.14.cloned.1.call-start = ((), (), s32[]{:S(2)}) async-start(), calls=%async_computation.4 | async-start | bytes 1310720 | tf_op jit(solution)/shard_map/all_gather | solution.py:39
  88.2 594.0 %all-gather.12.cloned.1.call-start = ((), (), s32[]{:S(2)}) async-start(), calls=%async_computation.3 | async-start | bytes 8519680 | tf_op jit(solution)/shard_map/all_gather | solution.py:32
  349.8 559.8 %all-gather.16.cloned.1.call-start = ((), (), s32[]{:S(2)}) async-start(), calls=%async_computation.5 | async-start | bytes 5242880 | tf_op jit(solution)/shard_map/all_gather | solution.py:39
  671.8 6.6 copy-start.2
  814.4 112.7 %all-to-all-start.1 = ((bf16[4,256,512]{1,2,0:T(8,128)(2,1)}), bf16[4,256,512]{1,2,0:T(8,128)(2,1)S(1)}, u32[]{:S(2)}, u32[]{:S(2)}) async-start(bf16[4,256,512]{1,2,0:T(8,128)(2,1)} %broadcast_in_dim.59), calls=%async_computation.1 | async-start | bytes 2097152 | tf_op jit(solution)/shard_map/all_to_all | solution.py:15
  909.7 21.6 %copy-start.1 = (s32[16384]{0:T(1024)S(1)}, s32[16384]{0:T(1024)}, u32[]{:S(2)}) copy-start(s32[16384]{0:T(1024)} %param.12) | copy-start | bytes 196612
Sparse Core Ops, SparseCore 0:
  9.1 334.8 all-gather.9
  345.8 63.5 all-gather.13
  411.1 267.4 all-gather.11
  680.2 121.1 all-gather.15
where the time goes:
time: 940 us; the launch traced here: 938 us
  blocking collectives  382 us (41%)
  waiting for transfers between devices  261 us (28%)
  matrix products  106 us (11%)
  starting transfers between devices  105 us (11%)
  local copies, waits for them, and re-layouts  39.1 us (4%)
  other arithmetic  27.8 us (3%)
  between operations  13.3 us (1%)
    all_gather x2, waiting for transfers between devices, side_by_side(): filled = lax.all_gather(both, axis, axis=dim, tiled=True)  249 us
    all_gather x1, blocking collectives, on_device(): lax.all_gather(document, SEQ, axis=0, tiled=True)  160 us
    all_gather x1, blocking collectives, on_device(): lax.all_gather(order, SEQ, axis=0, tiled=True)  155 us
    all_to_all x2, starting transfers between devices, sent_to_all(): return lax.all_to_all(copies, axis, split_axis=0, concat_axis=0, tiled=True)  105 us
    all_gather x1, blocking collectives, stacked_from(): blocks = lax.all_gather(blocks, axes[k])  67.4 us
    dot_general x32, matrix products, attend(): jnp.einsum('rkgc,ckd->rkgd', weights.astype(jnp.bfloat16), value_block, p...  50.5 us
    dot_general x32, matrix products, attend(): jnp.einsum('rkgd,ckd->rkgc', query, key_block, preferred_element_type=jnp...  43.4 us
  transfers between devices with their start and end apart: 6, of which 2 were waited for; matrix products, arithmetic and copies ran while one was open for 18% of the time, Pallas kernels for 0%

commit v1 on v0

--- a/solution.py
+++ b/solution.py
@@ -3,6 +3,7 @@
 from jax import lax
 from jax.sharding import Mesh
 from jax.sharding import PartitionSpec as P
+from jax.lax import all_to_all, axis_size
 
 HD = 128
 SEQ = ("seq_0", "seq_1", "seq_2")
@@ -110,9 +111,12 @@
         jnp.zeros((rows, groups_local, group, HD), jnp.float32),
     )
     carry = initial
+    lanes_choose = lambda vec: jnp.concatenate(
+        all_to_all(jnp.stack([vec for _ in range(axis_size(SEQ))], 0), SEQ, 0, 0), 0
+    )
     piece = (
         *side_by_side((key, value), SEQ, 0, 1),
-        lax.all_gather(order, SEQ, axis=0, tiled=True),
+        lanes_choose(order),
         lax.all_gather(document, SEQ, axis=0, tiled=True),
     )
     count = piece[0].shape[0]

time: 940 us -> 886 us (0.943)
  blocking collectives: 382 us -> 228 us
  waiting for transfers between devices: 261 us -> 411 us
  starting transfers between devices: 105 us -> 55.6 us
    all_gather x1 -> x0, blocking collectives: 155 us -> none  [on_device(): lax.all_gather(order, SEQ, axis=0, tiled=True)]
    all_gather x2, waiting for transfers between devices: 249 us -> 391 us  [side_by_side(): filled = lax.all_gather(both, axis, axis=dim, tiled=True)]
    all_to_all x2, starting transfers between devices: 105 us -> 47.3 us  [sent_to_all(): return lax.all_to_all(copies, axis, split_axis=0, concat_axis=0, tiled=True)]
  transfers between devices with their start and end apart: 6 -> 7, of which waited for: 2 -> 3; matrix products, arithmetic and copies ran while one was open for 18% -> 19% of each run, Pallas kernels for 0% -> 0%
where the time goes in v1:
time: 886 us; the launch traced here: 884 us
  waiting for transfers between devices  411 us (46%)
  blocking collectives  228 us (26%)
  matrix products  106 us (12%)
  starting transfers between devices  55.6 us (6%)
  local copies, waits for them, and re-layouts  39.7 us (4%)
  other arithmetic  27.8 us (3%)
  between operations  13.4 us (2%)
    all_gather x2, waiting for transfers between devices, side_by_side(): filled = lax.all_gather(both, axis, axis=dim, tiled=True)  391 us
    all_gather x1, blocking collectives, on_device(): lax.all_gather(document, SEQ, axis=0, tiled=True)  161 us
    all_gather x1, blocking collectives, stacked_from(): blocks = lax.all_gather(blocks, axes[k])  67.4 us
    dot_general x32, matrix products, attend(): jnp.einsum('rkgc,ckd->rkgd', weights.astype(jnp.bfloat16), value_block, p...  50.5 us
    all_to_all x2, starting transfers between devices, sent_to_all(): return lax.all_to_all(copies, axis, split_axis=0, concat_axis=0, tiled=True)  47.3 us
    dot_general x32, matrix products, attend(): jnp.einsum('rkgd,ckd->rkgc', query, key_block, preferred_element_type=jnp...  43.4 us
    all_to_all x2, waiting for transfers between devices, sent_to_all(): return lax.all_to_all(copies, axis, split_axis=0, concat_axis=0, tiled=True)  19.2 us
  transfers between devices with their start and end apart: 7, of which 3 were waited for; matrix products, arithmetic and copies ran while one was open for 19% of the time, Pallas kernels for 0%

profile of v1, /device:TPU:1, one launch (start us, length us, event | category | flops | bytes accessed | tf_op | source)
XLA Modules:
  0.0 883.7 jit_solution(17115614871665205951)
XLA Ops:
  6.5 1.6 pad_maximum_fusion.1
  8.1 2.6 broadcast_in_dim.58
  10.8 9.9 %all-to-all-start.1 = ((bf16[4,256,1024]{2,1,0:T(8,128)(2,1)}), bf16[4,256,1024]{2,1,0:T(8,128)(2,1)}, u32[]{:S(2)}, u32[]{:S(2)}) async-start(bf16[4,256,1024]{2,1,0:T(8,128)(2,1)} %broadcast_in_dim.58), calls=%async_computation.1 | async-start | bytes 4194304 | tf_op jit(solution)/shard_map/all_to_all | solution.py:16
  20.7 67.4 %all-gather = bf16[128,1024]{1,0:T(8,128)(2,1)} all-gather(bf16[32,1024]{1,0:T(8,128)(2,1)S(1)} %copy-done.5), channel_id=2, replica_groups=mesh['seq_0'=4,'seq_1'=4,'seq_2'=4,'tp'=4] {'seq_1'}, dimensions={0}, use_global_device_ids=true | all-gather | bytes 327680 | tf_op jit(solution)/shard_map/all_gather | solution.py:40
  88.3 1.7 gather_fusion
  90.0 2.9 copy.37
  93.5 1.7 fusion.21
  95.2 248.7 %all-gather.9.cloned.1.call-done = bf16[4096,768]{1,0:T(8,128)(2,1)} async-done(((bf16[64,768]{1,0:T(8,128)(2,1)}), bf16[4096,768]{1,0:T(8,128)(2,1)}) %all-gather.9.cloned.1.call-update) | async-done | bytes 6291472 | tf_op jit(solution)/shard_map/all_gather | solution.py:33
  343.9 2.4 convolution_bitcast_fusion.1
  346.7 2.4 fusion.22
  350.5 8.3 all-to-all-start
  358.9 160.5 %all-gather.3 = s32[64,1,256]{2,1,0:T(1,128)S(1)} all-gather(s32[1,1,256]{2,1,0:T(1,128)S(1)} %bitcast.139), channel_id=1, replica_groups=mesh['seq_0'=4,'seq_1'=4,'seq_2'=4,'tp'=4] {'seq_0','seq_1','seq_2'}, dimensions={0}, use_global_device_ids=true | all-gather | bytes 66560 | tf_op jit(solution)/shard_map/all_gather | solution.py:120
  520.2 1.7 multiply_convert_fusion
  521.9 4.5 slice_bitcast_fusion
  526.4 6.5 copy.39
  532.9 3.5 fusion.36
  536.7 142.6 %all-gather.11.cloned.1.call-done = bf16[16384,2,128]{0,2,1:T(8,128)(2,1)} async-done(((bf16[256,2,128]{0,2,1:T(8,128)(2,1)}), bf16[16384,2,128]{0,2,1:T(8,128)(2,1)}) %all-gather.11.cloned.1.call-update) | async-done | bytes 8388624 | tf_op jit(solution)/shard_map/all_gather | solution.py:33
  679.3 5.1 fusion.34
  684.4 2.5 copy.52
  686.9 6.4 copy.48
  693.3 117.1 %while.15 = (s32[]{:T(128)}, f32[256,1,4]{0,2,1:T(4,128)S(1)}, f32[256,1,4]{0,2,1:T(4,128)S(1)}, f32[256,1,4,128]{0,3,2,1:T(8,128)S(1)}, s32[32,512]{1,0:T(8,128...) while((s32[]{:T(128)}, f32[256,1,4]{0,2,1:T(4,128)S(1)}, ...), condition=%wide.region_4.5_spmd.clone, body=%wide.region_1.4_spmd.clone.sunk | while | flops 273428480 | bytes 8476829 | solution.py:124
  695.3 1.6 fusion.56
  699.0 1.6 fusion.56
  702.6 1.6 fusion.56
  706.3 1.6 fusion.56
  709.9 1.6 fusion.56
  713.6 1.6 fusion.56
  717.3 1.6 fusion.56
  720.9 1.6 fusion.56
  722.8 1.4 fusion.52
  724.6 1.6 fusion.56
  728.2 1.6 fusion.56
  731.9 1.6 fusion.56
  733.8 1.4 fusion.52
  735.6 1.6 fusion.56
  737.4 1.4 fusion.52
  739.2 1.6 fusion.56
  742.9 1.6 fusion.56
  744.8 1.4 fusion.52
  746.6 1.6 fusion.56
  748.4 1.4 fusion.52
  750.2 1.6 fusion.56
  753.9 1.6 fusion.56
  757.5 1.6 fusion.56
  759.4 1.4 fusion.52
  761.2 1.6 fusion.56
  764.9 1.6 fusion.56
  768.5 1.6 fusion.56
  772.2 1.6 fusion.56
  775.8 1.6 fusion.56
  779.5 1.6 fusion.56
  783.1 1.6 fusion.56
  786.8 1.6 fusion.56
  790.5 1.6 fusion.56
  794.1 1.6 fusion.56
  796.0 1.4 fusion.52
  797.8 1.6 fusion.56
  801.4 1.6 fusion.56
  805.1 1.6 fusion.56
  808.7 1.6 fusion.56
  811.5 37.3 %all-to-all-start.2 = ((bf16[4,256,512]{1,2,0:T(8,128)(2,1)}), bf16[4,256,512]{1,2,0:T(8,128)(2,1)S(1)}, u32[]{:S(2)}, u32[]{:S(2)}) async-start(bf16[4,256,512]{1,2,0:T(8,128)(2,1)} %broadcast_in_dim.59), calls=%async_computation.2 | async-start | bytes 2097152 | tf_op jit(solution)/shard_map/all_to_all | solution.py:16
  848.8 5.0 copy.44
  853.8 19.2 %all-to-all-done.2 = bf16[4,256,512]{1,2,0:T(8,128)(2,1)S(1)} async-done(((bf16[4,256,512]{1,2,0:T(8,128)(2,1)}), bf16[4,256,512]{1,2,0:T(8,128)(2,1)S(1)}, u32[]{:S(2)}, u32[]{:S(2)}) %all-to-all-start.2) | async-done | bytes 1048608 | tf_op jit(solution)/shard_map/all_to_all | solution.py:16
  872.9 4.3 convolution_convert_fusion
  (296 shorter events, 59.4 us)
Async XLA Ops:
  6.5 81.7 %copy-start = (s32[16384]{0:T(1024)S(1)}, s32[16384]{0:T(1024)}, u32[]{:S(2)}) copy-start(s32[16384]{0:T(1024)} %param.12) | copy-start | bytes 196612
  6.5 14.2 %copy-start.5 = (bf16[32,1024]{1,0:T(8,128)(2,1)S(1)}, bf16[32,1024]{1,0:T(8,128)(2,1)}, u32[]{:S(2)}) copy-start(bf16[32,1024]{1,0:T(8,128)(2,1)} %param.17) | copy-start | bytes 196612
  6.5 81.7 %copy-start.3 = (s32[256]{0:T(256)S(1)}, s32[256]{0:T(256)}, u32[]{:S(2)}) copy-start(s32[256]{0:T(256)} %param.11) | copy-start | bytes 3076
  6.5 337.4 %all-gather.9.cloned.1.call-start = ((), (), s32[]{:S(2)}) async-start(), calls=%async_computation.3 | async-start | bytes 6389760 | tf_op jit(solution)/shard_map/all_gather | solution.py:33
  10.8 79.3 %all-to-all-start.1 = ((bf16[4,256,1024]{2,1,0:T(8,128)(2,1)}), bf16[4,256,1024]{2,1,0:T(8,128)(2,1)}, u32[]{:S(2)}, u32[]{:S(2)}) async-start(bf16[4,256,1024]{2,1,0:T(8,128)(2,1)} %broadcast_in_dim.58), calls=%async_computation.1 | async-start | bytes 4194304 | tf_op jit(solution)/shard_map/all_to_all | solution.py:16
  20.7 72.8 %copy-start.4 = (f32[4096]{0:T(1024)S(1)}, f32[4096]{0:T(1024)}, u32[]{:S(2)}) copy-start(f32[4096]{0:T(1024)} %param.13) | copy-start | bytes 49156
  20.7 499.4 %all-gather.13.cloned.1.call-start = ((), (), s32[]{:S(2)}) async-start(), calls=%async_computation.5 | async-start | bytes 1310720 | tf_op jit(solution)/shard_map/all_gather | solution.py:40
  88.2 591.1 %all-gather.11.cloned.1.call-start = ((), (), s32[]{:S(2)}) async-start(), calls=%async_computation.4 | async-start | bytes 8519680 | tf_op jit(solution)/shard_map/all_gather | solution.py:33
  350.5 169.4 %all-to-all-start = ((s32[64,1,256]{2,1,0:T(1,128)}), s32[64,1,256]{2,1,0:T(1,128)S(1)}, u32[]{:S(2)}, u32[]{:S(2)}) async-start(s32[64,1,256]{2,1,0:T(1,128)} %stack.2), calls=%async_computation | async-start | bytes 131072 | tf_op jit(solution)/shard_map/all_to_all | solution.py:115
  358.8 490.0 %all-gather.15.cloned.1.call-start = ((), (), s32[]{:S(2)}) async-start(), calls=%async_computation.6 | async-start | bytes 5242880 | tf_op jit(solution)/shard_map/all_gather | solution.py:40
  526.4 6.5 copy-start.2
  811.5 61.5 %all-to-all-start.2 = ((bf16[4,256,512]{1,2,0:T(8,128)(2,1)}), bf16[4,256,512]{1,2,0:T(8,128)(2,1)S(1)}, u32[]{:S(2)}, u32[]{:S(2)}) async-start(bf16[4,256,512]{1,2,0:T(8,128)(2,1)} %broadcast_in_dim.59), calls=%async_computation.2 | async-start | bytes 2097152 | tf_op jit(solution)/shard_map/all_to_all | solution.py:16
  848.8 28.4 %copy-start.1 = (s32[16384]{0:T(1024)S(1)}, s32[16384]{0:T(1024)}, u32[]{:S(2)}) copy-start(s32[16384]{0:T(1024)} %param.12) | copy-start | bytes 196612
Sparse Core Ops, SparseCore 0:
  9.1 334.7 all-gather.8
  345.7 63.8 all-gather.12
  411.4 267.9 all-gather.10
  681.0 80.5 all-gather.14
